TPU v7x, 256 devices: a whole 4x4x8 slice. The times are simulated.
256 devices in a mesh: dp: 4 (over z_hi, core), vocab: 64 (over y, z_lo, x).
Axes of the slice: x: 4, y: 4, z: 8 (z_hi: 2, z_lo: 4; z = z_hi * 4 + z_lo), core: 2. Of those that a mesh axis runs over, the one named last changes fastest.
Arguments:
- hidden: bfloat16 [2048, 4608], P(('dp', 'vocab')), may hold values from -6 to 6
- embedding: bfloat16 [32768, 4608], P('vocab'), may hold values from -0.25 to 0.25
- targets: int32 [2048], P('dp'), may hold values from 0 to 32767
- grammar_bits: int32 [2048, 1024], P('dp', 'vocab'), may hold values from -2147483648 to 2147483647, as said below
Outputs:
- token_loss: float32 [2048], P('dp')
- hidden_grad: float32 [2048, 4608], P(('dp', 'vocab'))
- embed_grad: float32 [32768, 4608], P('vocab', 'dp')
Inputs may be any that keep to these rules, and one draw needn't show every extreme that they name: `grammar_bits`: bit b of word k of a token's row stands for vocabulary entry 32 k + b. Each 128-entry block of a row is either drawn at random or all zero, with a share of zero blocks that differs from block to block of the vocabulary.
All inputs are finite; a program needn't handle non-finite values.
Results may differ from a plain program's by a relative error of at most 0.0023.
Values may be sent and summed in bfloat16 or wider, within the bound.
A program may use at most 128 MiB of HBM per device.

v0:
```python
import jax
import jax.numpy as jnp
from jax import lax
from jax.sharding import Mesh
from jax.sharding import PartitionSpec as P

VOCAB = ("vocab_0", "vocab_1", "vocab_2")
DP = ("dp_0", "dp_1")
DP_VOCAB = ("dp_0", "dp_1", "vocab_0", "vocab_1", "vocab_2")


softcap = 30.0


def in_order(tiles, dim):
    tiles = jnp.moveaxis(tiles, 0, dim)
    shape = tiles.shape
    return tiles.reshape(*shape[:dim], shape[dim] * shape[dim + 1], *shape[dim + 2 :])


def all_blocks(value, axes, sequence):
    tiles = value
    for k in sequence:
        tiles = lax.all_gather(tiles, axes[k])
    done = sequence[::-1]
    back = [done.index(k) for k in range(len(axes))]
    tiles = tiles.transpose(*back, *range(len(axes), tiles.ndim))
    return tiles.reshape(-1, *value.shape)


def whole_of(value, axes, sequence, dim):
    return in_order(all_blocks(value, axes, sequence), dim)


def sent_to_all(value, axis):
    copies = jnp.broadcast_to(value, (lax.axis_size(axis), *value.shape))
    return lax.all_to_all(copies, axis, split_axis=0, concat_axis=0, tiled=True)


def over_copies(value, axis):
    return sent_to_all(value, axis).sum(axis=0)


def together(arrays, axis):
    ends = [0]
    for a in arrays:
        ends.append(ends[-1] + a.size)
    running = over_copies(jnp.concatenate([a.ravel() for a in arrays]), axis)
    return tuple((running[b:e].reshape(a.shape) for a, b, e in zip(arrays, ends, ends[1:])))


def sum_in_order(tiles, axes, sequence):
    inside = tiles.shape[1:]
    tiles = tiles.reshape(*(lax.axis_size(a) for a in axes), *inside)
    tiles = jnp.moveaxis(tiles, sequence, range(len(axes))).reshape(-1, *inside)
    for k in sequence:
        tiles = lax.psum_scatter(tiles, axes[k], scatter_dimension=0, tiled=True)
    return tiles[0]


def in_blocks(value, dim, size):
    before, after = (value.shape[:dim], value.shape[dim + 1 :])
    return jnp.moveaxis(value.reshape(*before, size, -1, *after), dim, 0)


def sum_by_axis_2(value, axes, sequence, dim):
    size = lax.axis_size(axes)
    return sum_in_order(in_blocks(value, dim, size), axes, sequence)


def summed_on_arrival(value, axis, dim):
    tiles = in_blocks(value, dim, lax.axis_size(axis))
    arrived = lax.all_to_all(tiles, axis, split_axis=0, concat_axis=0, tiled=True)
    return arrived.sum(axis=0)


def summed_rows(value, axes, dim):
    far, near = axes
    tiles = in_blocks(value, dim, lax.axis_size(far))
    nearer = summed_on_arrival(tiles, near, dim + 1)
    arrived = lax.all_to_all(nearer, far, split_axis=0, concat_axis=0, tiled=True)
    return arrived.sum(axis=0)


def score_rows(rows_piece, embedding):
    return lax.dot_general(
        rows_piece, embedding, (((1,), (1,)), ((), ())), preferred_element_type=jnp.float32
    )


def on_device(hidden, embedding, targets, grammar_bits):
    vocab_local = embedding.shape[0]
    vocab_start = lax.axis_index(VOCAB) * vocab_local
    gathered = whole_of(hidden, VOCAB, (1, 0, 2), 0)
    scores = score_rows(gathered, embedding)
    row_count = scores.shape[0]
    capped = softcap * jnp.tanh(scores / softcap)
    shifts = jnp.arange(32, dtype=jnp.int32)
    unpacked = jnp.right_shift(grammar_bits[:, :, None], shifts[None, None, :]) & 1
    unpacked = unpacked.reshape(row_count, vocab_local)
    vocab_ids = vocab_start + jnp.arange(vocab_local, dtype=jnp.int32)
    onehot = vocab_ids[None, :] == targets[:, None]
    allowed = (unpacked == 1) | onehot
    local_total = jnp.sum(jnp.where(allowed, jnp.exp(capped), 0.0), axis=1)
    local_target = jnp.sum(jnp.where(onehot, capped, 0.0), axis=1)
    totals, target_logit = together((local_total, local_target), VOCAB)
    log_total = jnp.log(totals)
    token_loss = log_total - target_logit
    probability = jnp.where(allowed, jnp.exp(capped - log_total[:, None]), 0.0)
    softcap_slope = 1.0 - jnp.square(capped / softcap)
    dlogit = ((probability - onehot.astype(jnp.float32)) * softcap_slope).astype(jnp.bfloat16)
    hidden_grad = sum_by_axis_2(
        jnp.dot(dlogit, embedding, preferred_element_type=jnp.float32), VOCAB, (0, 2, 1), 0
    )
    term = lax.dot_general(
        dlogit, gathered, (((0,), (0,)), ((), ())), preferred_element_type=jnp.float32
    )
    embed_grad = summed_rows(term, ("dp_0", "dp_1"), 1)
    return (token_loss, hidden_grad, embed_grad)


def solution(mesh):
    split = Mesh(
        mesh.devices.reshape(2, 2, 4, 4, 4), ("dp_0", "dp_1", "vocab_0", "vocab_1", "vocab_2")
    )
    return jax.shard_map(
        on_device,
        mesh=split,
        in_specs=(P(DP_VOCAB, None), P(VOCAB, None), P(DP), P(DP, VOCAB)),
        out_specs=(P(DP), P(DP_VOCAB, None), P(VOCAB, DP)),
        check_vma=False,
    )
```

profile of v0, /device:TPU:2, one launch (start us, length us, event | category | flops | bytes accessed | tf_op | source)
XLA Modules:
  0.0 402.7 jit_solution(2432391461042032054)
XLA Ops:
  7.2 17.2 %all-gather = bf16[32,4608]{1,0:T(8,128)(2,1)} all-gather(bf16[8,4608]{1,0:T(8,128)(2,1)} %param.4), channel_id=2, replica_groups=mesh['dp_0'=2,'dp_1'=2,'vocab_0'=4,'vocab_1'=4,'vocab_2'=4] {'vocab_1'}, dimensions={0}, use_global_device_ids=true | all-gather | bytes 368640 | tf_op jit(solution)/shard_map/all_gather | solution.py:24
  24.5 27.7 %all-gather.6.cloned.1.call-done = bf16[16,8,4608]{2,1,0:T(8,128)(2,1)} async-done(((bf16[4,8,4608]{2,1,0:T(8,128)(2,1)}), bf16[16,8,4608]{2,1,0:T(8,128)(2,1)}) %all-gather.6.cloned.1.call-update) | async-done | bytes 1179664 | tf_op jit(solution)/shard_map/all_gather | solution.py:24
  52.3 0.1 shift_right_arithmetic.23
  52.4 56.8 %all-gather.8.cloned.1.call-done = bf16[16,4,8,4608]{3,2,1,0:T(8,128)(2,1)} async-done(((bf16[4,4,8,4608]{3,2,1,0:T(8,128)(2,1)}), bf16[16,4,8,4608]{3,2,1,0:T(8,128)(2,1)}) %all-gather.8.cloned.1.call-update) | async-done | bytes 4718608 | tf_op jit(solution)/shard_map/all_gather | solution.py:24
  109.2 3.0 copy.19
  112.2 0.6 slice-done.1
  112.8 3.0 select_reduce_fusion
  115.9 0.1 broadcast_in_dim.15
  116.0 21.9 %all_to_all.16 = f32[64,1,1024]{2,1,0:T(1,128)S(1)} all-to-all(f32[64,1,1024]{2,1,0:T(1,128)S(1)} %broadcast_in_dim.15), channel_id=1, replica_groups=mesh['dp_0'=2,'dp_1'=2,'vocab_0'=4,'vocab_1'=4,'vocab_2'=4] {'vocab_0','..., dimensions={0} | all-to-all | bytes 524288 | tf_op jit(solution)/shard_map/all_to_all | solution.py:37
  137.9 0.2 reduce_sum.47
  138.1 0.6 slice_log_fusion
  138.7 5.1 %fusion.10 = f32[512,4608]{1,0:T(8,128)S(1)} fusion(bf16[512,4608]{1,0:T(8,128)(2,1)} %param.5, f32[512,512]{0,1:T(8,128)S(1)} %get-tuple-element.8, pred[512,512]{0,1:T(32,128)(4,1)S(1)} %get-tuple-element.5, f32[512]{0:T(512)S(1)} %get-tuple-element.6, s32[512]{0:T(512)S(1)} %copy-done.2, s32[512]{0:T(512)S(1)} %iota_add_fusion), kind=kOutput, calls=%fused_computation.20 | convolution fusion | flops 2418540544 | bytes 15472640 | tf_op jit(solution)/shard_map/dot_general | solution.py:113
  143.8 4.2 %copy.21 = f32[4,4,4,8,4608]{4,3,2,1,0:T(8,128)} copy(f32[4,4,4,8,4608]{4,3,1,2,0:T(8,128)S(1)} %bitcast.43) | data formatting | bytes 18874368 | tf_op jit(solution)/shard_map/transpose | solution.py:55
  148.0 0.0 reduce-scatter.6.cloned.1.call-start
  148.1 87.6 %reduce-scatter.4.cloned.1.call-done = f32[16,8,4608]{2,1,0:T(8,128)} async-done(((f32[64,8,4608]{2,1,0:T(8,128)}), f32[16,8,4608]{2,1,0:T(8,128)}) %reduce-scatter.4.cloned.1.call-update) | async-done | bytes 2359312 | tf_op jit(solution)/shard_map/reduce_scatter | solution.py:57
  235.7 6.7 %copy.22 = bf16[4608,512]{1,0:T(8,128)(2,1)} copy(bf16[4608,512]{0,1:T(8,128)(2,1)} %bitcast.39) | data formatting | bytes 9437184 | tf_op jit(solution)/shard_map/dot_general | solution.py:115
  242.4 5.5 %fusion.7 = f32[512,2,2304]{2,0,1:T(8,128)S(1)} fusion(bf16[2,2304,512]{2,1,0:T(8,128)(2,1)} %bitcast.44, f32[512,512]{0,1:T(8,128)} %copy-done.1, pred[512,512]{0,1:T(32,128)(4,1)S(1)} %get-tuple-element.5, f32[512]{0:T(512)S(1)} %get-tuple-element.6, s32[512]{0:T(512)S(1)} %copy-done.2, s32[512]{0:T(512)S(1)} %iota_add_fusion), kind=kOutput, calls=%fused_computation.14 | convolution fusion | flops 2418540544 | bytes 15472640 | tf_op jit(solution)/shard_map/dot_general | solution.py:115
  247.9 0.6 copy.29
  248.5 12.7 %all_to_all.17 = f32[2,2,512,1152]{3,2,1,0:T(8,128)} all-to-all(f32[2,2,512,1152]{3,2,1,0:T(8,128)S(1)} %bitcast.42), channel_id=1, replica_groups=mesh['dp_0'=2,'dp_1'=2,'vocab_0'=4,'vocab_1'=4,'vocab_2'=4] {'dp_1'}, dimensions={0} | all-to-all | bytes 18874368 | tf_op jit(solution)/shard_map/all_to_all | solution.py:73
  261.2 7.1 %reduce_sum.48 = f32[2,512,1152]{2,1,0:T(8,128)} reduce(f32[2,2,512,1152]{3,2,1,0:T(8,128)} %all_to_all.17, f32[]{:T(128)} %constant.28.clone.1), dimensions={0}, to_apply=%region_6.7 | reduce | flops 1179648 | bytes 14155780 | tf_op jit(solution)/shard_map/reduce_sum | solution.py:74
  268.3 7.0 %all-to-all-start.2 = ((f32[2,512,1152]{2,1,0:T(8,128)}), f32[2,512,1152]{2,1,0:T(8,128)}, u32[]{:S(2)}, u32[]{:S(2)}) async-start(f32[2,512,1152]{2,1,0:T(8,128)} %reduce_sum.48), calls=%async_computation.5 | async-start | bytes 9437184 | tf_op jit(solution)/shard_map/all_to_all | solution.py:81
  275.4 0.6 reduce-scatter.8.cloned.1.call-update
  275.9 115.9 %all-to-all-done.2 = f32[2,512,1152]{2,1,0:T(8,128)} async-done(((f32[2,512,1152]{2,1,0:T(8,128)}), f32[2,512,1152]{2,1,0:T(8,128)}, u32[]{:S(2)}, u32[]{:S(2)}) %all-to-all-start.2) | async-done | bytes 4718624 | tf_op jit(solution)/shard_map/all_to_all | solution.py:81
  391.8 4.3 %reduce_sum.49 = f32[512,1152]{1,0:T(8,128)} reduce(f32[2,512,1152]{2,1,0:T(8,128)} %all-to-all-done.2, f32[]{:T(128)} %constant.28.clone.1), dimensions={0}, to_apply=%region_7.8 | reduce | flops 589824 | bytes 7077892 | tf_op jit(solution)/shard_map/reduce_sum | solution.py:82
  (25 shorter events, 0.2 us)
Async XLA Ops:
  7.2 45.1 %all-gather.6.cloned.1.call-start = ((), (), s32[]{:S(2)}) async-start(), calls=%async_computation.9 | async-start | bytes 1474560 | tf_op jit(solution)/shard_map/all_gather | solution.py:24
  24.4 84.8 %all-gather.8.cloned.1.call-start = ((), (), s32[]{:S(2)}) async-start(), calls=%async_computation.10 | async-start | bytes 5898240 | tf_op jit(solution)/shard_map/all_gather | solution.py:24
  52.2 60.0 %slice-start = ((s8[4718592]{0:T(1024)(128)(4,1)}), s8[524288]{0:T(1024)(128)(4,1)S(1)}, s32[]{:S(2)}) async-start(s8[4718592]{0:T(1024)(128)(4,1)} %bitcast.45), calls=%async_computation.11 | async-start | bytes 1048576
  52.2 183.5 %reduce-scatter.4.cloned.1.call-start = ((), (), s32[]{:S(2)}) async-start(), calls=%async_computation.6 | async-start | bytes 11796480 | tf_op jit(solution)/shard_map/reduce_scatter | solution.py:57
  109.2 3.6 slice-start.1
  109.2 3.6 copy-start.2
  109.2 3.6 copy-start.3
  112.2 3.7 copy-start
  115.9 27.9 %copy-start.1 = (f32[512,512]{0,1:T(8,128)}, f32[512,512]{0,1:T(8,128)S(1)}, u32[]{:S(2)}) copy-start(f32[512,512]{0,1:T(8,128)S(1)} %get-tuple-element.8) | copy-start | bytes 3145732
  148.0 127.3 %reduce-scatter.6.cloned.1.call-start = ((), (), s32[]{:S(2)}) async-start(), calls=%async_computation.7 | async-start | bytes 2949120 | tf_op jit(solution)/shard_map/reduce_scatter | solution.py:57
  268.3 123.5 %all-to-all-start.2 = ((f32[2,512,1152]{2,1,0:T(8,128)}), f32[2,512,1152]{2,1,0:T(8,128)}, u32[]{:S(2)}, u32[]{:S(2)}) async-start(f32[2,512,1152]{2,1,0:T(8,128)} %reduce_sum.48), calls=%async_computation.5 | async-start | bytes 9437184 | tf_op jit(solution)/shard_map/all_to_all | solution.py:81
  275.3 120.8 %reduce-scatter.8.cloned.1.call-start = ((), (), s32[]{:S(2)}) async-start(), calls=%async_computation.8 | async-start | bytes 737280 | tf_op jit(solution)/shard_map/reduce_scatter | solution.py:57
Sparse Core Ops, SparseCore 0:
  24.5 27.6 all-gather.5
  54.0 55.1 all-gather.7
  148.1 87.5 reduce-scatter.3
  238.1 32.9 reduce-scatter.5
  278.9 39.1 reduce-scatter.7
where the time goes:
time: 403 us
  waiting for transfers between devices  289 us (72%)
  blocking collectives  51.8 us (13%)
  local copies, waits for them, and re-layouts  15.3 us (4%)
  between operations  13.9 us (3%)
  matrix products  13.6 us (3%)
  other arithmetic  12.2 us (3%)
  starting transfers between devices  7.18 us (2%)
    all_to_all x1, waiting for transfers between devices, summed_rows(): lax.all_to_all(nearer, far, split_axis=0, concat_axis=0, tiled=True)  116 us
    reduce_scatter x3, waiting for transfers between devices, sum_in_order(): tiles = lax.psum_scatter(tiles, axes[k], scatter_dimension=0, tiled=True)  87.6 us
    all_gather x2, waiting for transfers between devices, all_blocks(): tiles = lax.all_gather(tiles, axes[k])  84.6 us
    all_to_all x1, blocking collectives, sent_to_all(): return lax.all_to_all(copies, axis, split_axis=0, concat_axis=0, tiled=True)  21.9 us
    all_gather x1, blocking collectives, all_blocks(): tiles = lax.all_gather(tiles, axes[k])  17.2 us
    all_to_all x1, blocking collectives, summed_on_arrival(): lax.all_to_all(tiles, axis, split_axis=0, concat_axis=0, tiled=True)  12.7 us
  transfers between devices with their start and end apart: 6, of which 4 were waited for; matrix products, arithmetic and copies ran while one was open for 6% of the time, Pallas kernels for 0%

commit v1 on v0

v1 whole, which is shorter than its diff:
```python
import functools

import jax
import jax.numpy as jnp
from jax import lax
from jax.experimental import pallas as pl
from jax.experimental.pallas import tpu as pltpu
from jax.sharding import Mesh
from jax.sharding import PartitionSpec as P

AXES = ("dp_0", "dp_1", "vocab_0", "vocab_1", "vocab_2")
VOCAB = ("vocab_0", "vocab_1", "vocab_2")
DP = ("dp_0", "dp_1")
HALF, CORE, Y, Z, X = AXES
MESH = pl.DeviceIdType.MESH
N = 4
ROWS = 8
softcap = 30.0
F32, BF16 = jnp.float32, jnp.bfloat16


def fold(k):
    return lax.rem(k, N)


def masks(words, targets, first_id):
    rows = 32 * words.shape[0]
    bit = lax.broadcasted_iota(jnp.int32, (32, words.shape[1]), 0)
    spread = [jnp.right_shift(words[k : k + 1], bit) & 1 for k in range(words.shape[0])]
    unpacked = spread[0] if len(spread) == 1 else jnp.concatenate(spread, axis=0)
    ids = first_id + lax.broadcasted_iota(jnp.int32, (rows, words.shape[1]), 0)
    onehot = ids == targets
    return (unpacked == 1) | onehot, onehot


class Mail:
    def __init__(self, send_sem, recv_sem):
        self.send_sem, self.recv_sem = send_sem, recv_sem
        self.count = 0
        self.sent = []

    def post(self, src, dst, device):
        k = self.count
        self.count += 1
        copy = pltpu.make_async_remote_copy(
            src_ref=src,
            dst_ref=dst,
            send_sem=self.send_sem.at[k],
            recv_sem=self.recv_sem.at[k],
            device_id=device,
            device_id_type=MESH,
        )
        copy.start()
        self.sent.append(copy)
        return copy

    def close(self):
        for copy in self.sent:
            copy.wait_send()


class Gather:
    def __init__(self, mail, view, at, first, second):
        self.mail, self.view = mail, view
        self.first, self.second = first, second
        self.u, self.v = at[first], at[second]
        self.planes = []

    def ref(self, u, v, start=0, size=N):
        y, x = (u, v) if self.first == Y else (v, u)
        return self.view(y, pl.ds(start, size), x)

    def near(self, axis, ref):
        k = self.u if axis == self.first else self.v
        return [self.mail.post(ref, ref, {axis: fold(k + d)}) for d in (1, N - 1)]

    def along_first(self):
        self.plus, self.minus = self.near(self.first, self.ref(self.u, self.v))

    def plane(self, d):
        p = fold(self.u + d)
        self.planes.append((p, self.near(self.second, self.ref(p, self.v))))

    def relay_first(self):
        before, after = fold(self.u + N - 1), fold(self.u + 1)
        self.plus.wait_recv()
        low = self.ref(before, self.v, 0, 2)
        self.far = [self.mail.post(low, low, {self.first: after})]
        self.minus.wait_recv()
        high = self.ref(after, self.v, 2, 2)
        self.far.append(self.mail.post(high, high, {self.first: before}))
        self.relays = []

    def far_first(self):
        for copy in self.far:
            copy.wait_recv()

    def relay_second(self, k):
        before, after = fold(self.v + N - 1), fold(self.v + 1)
        p, (plus, minus) = self.planes[k]
        plus.wait_recv()
        low = self.ref(p, before, 0, 2)
        self.relays.append(self.mail.post(low, low, {self.second: after}))
        minus.wait_recv()
        high = self.ref(p, after, 2, 2)
        self.relays.append(self.mail.post(high, high, {self.second: before}))

    def finish(self):
        for copy in self.relays:
            copy.wait_recv()


class Reduce:
    def __init__(self, mail, part, boxes, at, first, second, out, columns):
        self.mail, self.part, self.at = mail, part, at
        self.send1, self.recv1, self.mid, self.send2, self.recv2, self.last, self.send3, self.recv3 = boxes
        self.first, self.second = first, second
        self.u, self.w = at[first], at[second]
        self.out, self.columns = out, columns

    def partial(self, u, w, start):
        y, x = (w, u) if self.first == X else (u, w)
        return self.part[y, pl.ds(start, 2), x]

    def post1(self, k, d):
        return self.mail.post(self.send1.at[k], self.recv1.at[k], {self.first: fold(self.u + d)})

    def post2(self, k, d):
        return self.mail.post(self.send2.at[k], self.recv2.at[k], {self.second: fold(self.w + d)})

    def open1(self):
        self.one = []
        plan = ((2, 0, 1), (2, 2, N - 1), (1, 2, 1), (N - 1, 0, N - 1))
        for k, (to, start, d) in enumerate(plan):
            u = fold(self.u + to)

            def stage(w, _):
                self.send1[k, w] = self.partial(u, w, start).astype(BF16)
                return _

            lax.fori_loop(0, N, stage, 0)
            self.one.append(self.post1(k, d))

    def relay1(self):
        for k, to, start in ((0, 1, 0), (1, N - 1, 2)):
            self.one[k].wait_recv()
            u = fold(self.u + to)

            def stage(w, _):
                total = self.partial(u, w, start) + self.recv1[k, w].astype(F32)
                self.send1[4 + k, w] = total.astype(BF16)
                return _

            lax.fori_loop(0, N, stage, 0)
            self.one.append(self.post1(4 + k, to))

    def open2(self):
        for k in (2, 3, 4, 5):
            self.one[k].wait_recv()

        def total(w, _):
            self.mid[w, 0:2] = (
                self.partial(self.u, w, 0) + self.recv1[3, w].astype(F32) + self.recv1[4, w].astype(F32)
            )
            self.mid[w, 2:4] = (
                self.partial(self.u, w, 2) + self.recv1[2, w].astype(F32) + self.recv1[5, w].astype(F32)
            )
            return _

        lax.fori_loop(0, N, total, 0)
        self.two = []
        plan = ((2, 0, 1), (2, 2, N - 1), (1, 2, 1), (N - 1, 0, N - 1))
        for k, (to, start, d) in enumerate(plan):
            self.send2[k] = self.mid[fold(self.w + to), start : start + 2].astype(self.send2.dtype)
            self.two.append(self.post2(k, d))

    def relay2(self):
        for k, to, start in ((0, 1, 0), (1, N - 1, 2)):
            self.two[k].wait_recv()
            total = self.mid[fold(self.w + to), start : start + 2] + self.recv2[k].astype(F32)
            self.send2[4 + k] = total.astype(self.send2.dtype)
            self.two.append(self.post2(4 + k, to))

    def open3(self):
        for k in (2, 3, 4, 5):
            self.two[k].wait_recv()
        self.last[0:2] = self.mid[self.w, 0:2] + self.recv2[3].astype(F32) + self.recv2[4].astype(F32)
        self.last[2:4] = self.mid[self.w, 2:4] + self.recv2[2].astype(F32) + self.recv2[5].astype(F32)
        self.three = []
        for d in range(1, N):
            z = fold(self.at[Z] + d)
            self.send3[d - 1] = self.last[z].astype(BF16)
            self.three.append(self.mail.post(self.send3.at[d - 1], self.recv3.at[d - 1], {Z: z}))

    def finish(self):
        total = self.last[self.at[Z]]
        for d in range(1, N):
            self.three[d - 1].wait_recv()
            total += self.recv3[d - 1].astype(F32)
        self.out[:, self.columns] = total


def kernel(
    hidden, words, targets, embedding_hbm,
    loss, hidden_grad, embed_grad,
    tokens, extra, sibling, embedding, scores, dlogits, by_token, part, sums,
    send1, recv1, mid, send2, recv2, last, send3, recv3,
    load_sem, send_sem, recv_sem,
):
    at = {a: lax.axis_index(a) for a in AXES}
    half, core, y, z, x = (at[a] for a in AXES)
    width = hidden.shape[1]
    vocab_local = embedding.shape[0]
    group = tokens.shape[0] * tokens.shape[1] * tokens.shape[2] * ROWS
    color, share, lane = width // 2, width // 4, width // 4
    partner = {HALF: 1 - half}
    across = {HALF: 1 - half, CORE: 1 - core}
    other = {CORE: 1 - core}
    vocab_start = ((y * N + z) * N + x) * vocab_local

    load = pltpu.make_async_copy(embedding_hbm, embedding, load_sem)
    load.start()
    barrier = pltpu.get_barrier_semaphore()
    greeted = [{a: fold(at[a] + d)} for a in (X, Y, Z) for d in range(1, N)] + [partner, across, other]
    for device in greeted:
        pl.semaphore_signal(barrier, inc=1, device_id=device, device_id_type=MESH)
    pl.semaphore_wait(barrier, len(greeted))

    mail = Mail(send_sem, recv_sem)
    own = [mail.post(hidden, tokens.at[y, z, x], {Z: fold(z + d)}) for d in (1, N - 1, 2)]

    def share_of(h, c):
        return pl.ds(pl.multiple_of((2 * h + c) * share, 128), share)

    crossed = [
        mail.post(hidden.at[:, share_of(1 - half, core)], extra.at[0, y, z, x], partner),
        mail.post(hidden.at[:, share_of(1 - half, 1 - core)], extra.at[1, y, z, x], across),
    ]
    tokens[y, z, x] = hidden[...]

    def main_view(start):
        return lambda yy, zz, xx: tokens.at[yy, zz, xx, :, pl.ds(start, color)]

    def extra_view(k):
        return lambda yy, zz, xx: extra.at[k, yy, zz, xx]

    mains = [Gather(mail, main_view(0), at, Y, X), Gather(mail, main_view(color), at, X, Y)]
    extras = [Gather(mail, extra_view(0), at, Y, X), Gather(mail, extra_view(1), at, X, Y)]

    for copy in own:
        copy.wait_recv()
    for g in mains:
        g.along_first()
    for g in mains:
        g.plane(0)
    for copy in crossed:
        copy.wait_recv()
    lifted = [mail.post(extra.at[:, y, z, x], extra.at[:, y, z, x], {Z: fold(z + d)}) for d in (1, N - 1, 2)]
    for g in mains:
        g.relay_first()
    for g in mains:
        g.plane(N - 1)
        g.plane(1)
    for g in mains:
        g.relay_second(0)
    for g in mains:
        g.far_first()
        g.plane(2)
    for copy in lifted:
        copy.wait_recv()
    for g in mains:
        g.relay_second(1)
    for g in mains:
        g.relay_second(2)
    for g in extras:
        g.along_first()
    for g in extras:
        g.plane(0)
    for g in mains:
        g.relay_second(3)
    for g in mains:
        g.finish()
    load.wait()

    to_sibling = mail.post(
        tokens.at[:, :, :, :, share_of(half, 1 - core)], sibling.at[...], other
    )

    block = group // 2

    def score(k, _):
        rows = tokens[pl.ds(2 * k, 2)].reshape(block, width)
        scores[k] = lax.dot_general(
            embedding[...], rows, (((1,), (1,)), ((), ())), preferred_element_type=F32
        )
        return _

    lax.fori_loop(0, 2, score, 0)

    for g in extras:
        g.relay_first()

    def cap(w, carry):
        total, target = carry
        rows = pl.ds(pl.multiple_of(w * 32, 32), 32)
        raw = jnp.concatenate([scores[0, rows], scores[1, rows]], axis=1)
        capped = softcap * jnp.tanh(raw / softcap)
        scores[0, rows] = capped[:, :block]
        scores[1, rows] = capped[:, block:]
        allowed, onehot = masks(words[pl.ds(w, 1)], targets[...], vocab_start + w * 32)
        total += jnp.where(allowed, jnp.exp(capped), 0.0).reshape(4, 8, group).sum(axis=0)
        target += jnp.where(onehot, capped, 0.0).reshape(4, 8, group).sum(axis=0)
        return total, target

    zero = jnp.zeros((8, group), F32)
    total, target = lax.fori_loop(0, vocab_local // 32, cap, (zero, zero))
    total = total.sum(axis=0, keepdims=True)
    target = target.sum(axis=0, keepdims=True)
    for step, axis in enumerate((X, Y, Z)):
        me = at[axis]
        sums[step, me, 0:1] = total
        sums[step, me, 1:2] = target
        swaps = [
            mail.post(sums.at[step, me], sums.at[step, me], {axis: fold(me + d)}) for d in range(1, N)
        ]
        for copy in swaps:
            copy.wait_recv()
        both = sums[step].sum(axis=0)
        total, target = both[0:1], both[1:2]
    log_total = jnp.log(total)
    loss[...] = log_total - target

    def differentiate(k, _):
        rows = pl.ds(pl.multiple_of(k * 128, 128), 128)
        capped = jnp.concatenate([scores[0, rows], scores[1, rows]], axis=1)
        allowed, onehot = masks(words[pl.ds(4 * k, 4)], targets[...], vocab_start + k * 128)
        probability = jnp.where(allowed, jnp.exp(capped - log_total), 0.0)
        slope = 1.0 - jnp.square(capped / softcap)
        value = (probability - jnp.where(onehot, 1.0, 0.0)) * slope
        dlogits[0, rows] = value.astype(BF16)
        by_token[:, rows] = value.T.astype(BF16)
        return _

    for k in range(vocab_local // 128):
        differentiate(k, 0)

    around = mail.post(dlogits.at[0], dlogits.at[2], partner)
    beside = mail.post(dlogits.at[0], dlogits.at[1], other)

    tile = lane // 3

    def product(k):
        def piece(j, _):
            source = pl.ds(pl.multiple_of(k * lane + j * tile, 128), tile)
            columns = pl.ds(pl.multiple_of(j * tile, 128), tile)
            value = jnp.dot(by_token[...], embedding[:, source], preferred_element_type=F32)
            part[k, :, :, :, :, columns] = value.reshape(N, N, N, ROWS, tile)
            return _

        lax.fori_loop(0, 3, piece, 0)

    lanes = []
    for k, (first, second) in enumerate(((X, Y), (X, Y), (Y, X), (Y, X))):
        boxes = [b.at[k] for b in (send1, recv1, mid, send2, recv2, last, send3, recv3)]
        lanes.append(
            Reduce(mail, part.at[k], boxes, at, first, second, hidden_grad, pl.ds(k * lane, lane))
        )
    early, late = (lanes[0], lanes[2]), (lanes[1], lanes[3])

    def grad(k, source, begin):
        def piece(j, _):
            columns = pl.ds(pl.multiple_of(j * tile, 128), tile)
            value = jnp.dot(
                dlogits[k], source(j).reshape(group, tile), preferred_element_type=F32
            )
            if begin:
                embed_grad[:, columns] = value
            else:
                embed_grad[:, columns] += value
            return _

        lax.fori_loop(0, 3, piece, 0)

    def columns_of(j):
        return pl.ds(pl.multiple_of(j * tile, 128), tile)

    def own_columns(j):
        return pl.ds(pl.multiple_of((2 * half + core) * share + j * tile, 128), tile)

    product(0)
    lanes[0].open1()
    product(2)
    lanes[2].open1()
    product(1)
    product(3)
    for r in early:
        r.relay1()
    for r in late:
        r.open1()
    grad(0, lambda j: tokens[:, :, :, :, own_columns(j)], True)
    for g in extras:
        g.plane(N - 1)
        g.plane(1)
    for g in extras:
        g.relay_second(0)
    for g in extras:
        g.far_first()
        g.plane(2)
    for r in early:
        r.open2()
    for r in late:
        r.relay1()
    beside.wait_recv()
    to_sibling.wait_recv()
    grad(1, lambda j: sibling[:, :, :, :, columns_of(j)], False)
    for r in early:
        r.relay2()
    for g in extras:
        g.relay_second(1)
        g.relay_second(2)
        g.relay_second(3)
    around.wait_recv()
    passed = mail.post(dlogits.at[2], dlogits.at[3], other)
    for r in late:
        r.open2()
    for r in early:
        r.open3()
    for r in late:
        r.relay2()
    for g in extras:
        g.finish()
    grad(2, lambda j: extra[0, :, :, :, :, columns_of(j)], False)
    for r in late:
        r.open3()
    passed.wait_recv()
    grad(3, lambda j: extra[1, :, :, :, :, columns_of(j)], False)
    for r in early + late:
        r.finish()
    mail.close()


def on_device(hidden, embedding, targets, grammar_bits):
    rows, width = hidden.shape
    vocab_local = embedding.shape[0]
    group = targets.shape[0]
    lane = width // 4
    vmem = pl.BlockSpec(memory_space=pltpu.VMEM)
    blocks = (N, N, N, ROWS)
    loss, hidden_grad, embed_grad = pl.pallas_call(
        kernel,
        out_shape=(
            jax.ShapeDtypeStruct((1, group), F32),
            jax.ShapeDtypeStruct((rows, width), F32),
            jax.ShapeDtypeStruct((vocab_local, lane), F32),
        ),
        in_specs=[vmem, vmem, vmem, pl.BlockSpec(memory_space=pl.ANY)],
        out_specs=(vmem, vmem, vmem),
        scratch_shapes=[
            pltpu.VMEM(blocks + (width,), BF16),
            pltpu.VMEM((2,) + blocks + (lane,), BF16),
            pltpu.VMEM(blocks + (lane,), BF16),
            pltpu.VMEM((vocab_local, width), BF16),
            pltpu.VMEM((2, vocab_local, group // 2), F32),
            pltpu.VMEM((4, vocab_local, group), BF16),
            pltpu.VMEM((group, vocab_local), BF16),
            pltpu.VMEM((4,) + blocks + (lane,), F32),
            pltpu.VMEM((3, N, 2, group), F32),
            pltpu.VMEM((4, 6, N, 2, ROWS, lane), BF16),
            pltpu.VMEM((4, 6, N, 2, ROWS, lane), BF16),
            pltpu.VMEM((4, N, N, ROWS, lane), F32),
            pltpu.VMEM((4, 6, 2, ROWS, lane), F32),
            pltpu.VMEM((4, 6, 2, ROWS, lane), F32),
            pltpu.VMEM((4, N, ROWS, lane), F32),
            pltpu.VMEM((4, N - 1, ROWS, lane), BF16),
            pltpu.VMEM((4, N - 1, ROWS, lane), BF16),
            pltpu.SemaphoreType.DMA,
            pltpu.SemaphoreType.DMA((170,)),
            pltpu.SemaphoreType.DMA((170,)),
        ],
        compiler_params=pltpu.CompilerParams(
            collective_id=0, has_side_effects=True, vmem_limit_bytes=67043328
        ),
        name="fused",
    )(hidden, grammar_bits.T, targets[None, :], embedding)
    return loss[0], hidden_grad, embed_grad


def solution(mesh):
    split = Mesh(mesh.devices.reshape(2, 2, 4, 4, 4), AXES)
    return jax.shard_map(
        on_device,
        mesh=split,
        in_specs=(P(AXES, None), P(VOCAB, None), P(DP), P(DP, VOCAB)),
        out_specs=(P(DP), P(AXES, None), P(VOCAB, DP)),
        check_vma=False,
    )
```

time: 403 us -> 120 us (0.30)
  waiting for transfers between devices: 289 us -> 0 us
  Pallas kernels: 0 us -> 113 us
  blocking collectives: 51.8 us -> 0 us
  matrix products: 13.6 us -> 0 us
  between operations: 13.9 us -> 0.64 us
  other arithmetic: 12.2 us -> 0 us
  local copies, waits for them, and re-layouts: 15.3 us -> 6.04 us
  starting transfers between devices: 7.18 us -> 0 us
    all_to_all x1 -> x0, waiting for transfers between devices: 116 us -> none  [summed_rows(): lax.all_to_all(nearer, far, split_axis=0, concat_axis=0, tiled=True)]
    pallas_call x0 -> x1, Pallas kernels: none -> 113 us  [on_device(): pl.pallas_call(kernel, out_shape=(jax.ShapeDtypeStruct((1, group), F32),...]
    reduce_scatter x3 -> x0, waiting for transfers between devices: 87.6 us -> none  [sum_in_order(): tiles = lax.psum_scatter(tiles, axes[k], scatter_dimension=0, tiled=True)]
    all_gather x2 -> x0, waiting for transfers between devices: 84.6 us -> none  [all_blocks(): tiles = lax.all_gather(tiles, axes[k])]
    all_to_all x2 -> x0, blocking collectives: 34.6 us -> none  [the longest x1 21.9 us: sent_to_all(): return lax.all_to_all(copies, axis, split_axis=0, concat_axis=0, tiled=True)]
    all_gather x1 -> x0, blocking collectives: 17.2 us -> none  [all_blocks(): tiles = lax.all_gather(tiles, axes[k])]
    dot_general x3 -> x0, matrix products: 13.6 us -> none  [the longest x1 5.48 us: on_device(): lax.dot_general(dlogit, gathered, (((0,), (0,)), ((), ())), preferred_ele...]
    reduce_sum x3 -> x0, other arithmetic: 11.6 us -> none  [the longest x1 7.13 us: summed_on_arrival(): return arrived.sum(axis=0)]
  transfers between devices with their start and end apart: 6 -> 0, of which waited for: 4 -> 0; matrix products, arithmetic and copies ran while one was open for 6% -> 0% of each run, Pallas kernels for 0% -> 0%
where the time goes in v1:
time: 120 us; the launch traced here: 119 us
  Pallas kernels  113 us (94%)
  local copies, waits for them, and re-layouts  6.04 us (5%)
    pallas_call x1, Pallas kernels, on_device(): pl.pallas_call(kernel, out_shape=(jax.ShapeDtypeStruct((1, group), F32),...  113 us
    unnamed x3, local copies, waits for them, and re-layouts  6.04 us

profile of v1, /device:TPU:2, one launch (start us, length us, event | category | flops | bytes accessed | tf_op | source)
XLA Modules:
  0.0 119.3 jit_solution(2137112505346541819)
XLA Ops:
  0.6 112.6 %fused.1 = (f32[1,512]{1,0:T(1,128)}, f32[8,4608]{1,0:T(8,128)}, f32[512,1152]{1,0:T(8,128)}) custom-call(bf16[8,4608]{1,0:T(8,128)(2,1)} %hidden.1, s32[16,512]{1,0:T(8,128)} %bitcast.3, s32[1,512]{1,0:T(1,128)} %bitcast.4, bf16[512,4608]{1,0:T(8,128)(2,1)} %embedding_hbm.1), custom_call_target="tpu_custom_call" | custom-call | tf_op jit(solution)/shard_map/fused/pallas_call | solution.py:449
  113.3 1.2 %copy.10 = f32[512]{0:T(512)} copy(f32[512]{0:T(512)} %bitcast.5) | data formatting | bytes 4096
  114.5 1.6 %copy.11 = f32[8,4608]{1,0:T(8,128)} copy(f32[8,4608]{1,0:T(8,128)} %get-tuple-element.13) | data formatting | bytes 294912
  116.1 3.2 %copy.12 = f32[512,1152]{1,0:T(8,128)} copy(f32[512,1152]{1,0:T(8,128)} %get-tuple-element.14) | data formatting | bytes 4718592

commit v2 on v1

v2 whole, which is shorter than its diff:
```python
import functools

import jax
import jax.numpy as jnp
from jax import lax
from jax.experimental import pallas as pl
from jax.experimental.pallas import tpu as pltpu
from jax.sharding import Mesh
from jax.sharding import PartitionSpec as P

AXES = ("dp_0", "dp_1", "vocab_0", "vocab_1", "vocab_2")
VOCAB = ("vocab_0", "vocab_1", "vocab_2")
DP = ("dp_0", "dp_1")
HALF, CORE, Y, Z, X = AXES
MESH = pl.DeviceIdType.MESH
N = 4
ROWS = 8
LANES = 3
softcap = 30.0
F32, BF16 = jnp.float32, jnp.bfloat16


def fold(k):
    return lax.rem(k, N)


def masks(words, targets, first_id):
    rows = 32 * words.shape[0]
    bit = lax.broadcasted_iota(jnp.int32, (32, words.shape[1]), 0)
    spread = [jnp.right_shift(words[k : k + 1], bit) & 1 for k in range(words.shape[0])]
    unpacked = spread[0] if len(spread) == 1 else jnp.concatenate(spread, axis=0)
    ids = first_id + lax.broadcasted_iota(jnp.int32, (rows, words.shape[1]), 0)
    onehot = ids == targets
    return (unpacked == 1) | onehot, onehot


class Mail:
    def __init__(self, send_sem, recv_sem):
        self.send_sem, self.recv_sem = send_sem, recv_sem
        self.count = 0
        self.sent = []

    def describe(self, src, dst, device, send, recv):
        return pltpu.make_async_remote_copy(
            src_ref=src,
            dst_ref=dst,
            send_sem=self.send_sem.at[send],
            recv_sem=self.recv_sem.at[recv],
            device_id=device,
            device_id_type=MESH,
        )

    def start(self, copy):
        copy.start()
        self.sent.append(copy)
        return copy

    def post(self, src, dst, device):
        k = self.count
        self.count += 1
        return self.start(self.describe(src, dst, device, k, k))

    def post_each(self, src, dst, axis, me, steps):
        base = self.count - 1
        self.count += N - 1
        for d in steps:
            self.start(self.describe(src, dst, {axis: fold(me + d)}, base + d, base + N - d))
        return [self.describe(src, dst, {axis: fold(me + d)}, base + d, base + d) for d in steps]

    def close(self):
        for copy in self.sent:
            copy.wait_send()


class Gather:
    def __init__(self, mail, view, at, first, second, span):
        self.mail, self.view, self.span = mail, view, span
        self.first, self.second = first, second
        self.u, self.v = at[first], at[second]
        self.relays = []
        self.planes = {}

    def ref(self, u, v, piece):
        y, x = (u, v) if self.first == Y else (v, u)
        return self.view(y, x, self.span[piece])

    def both(self, axis, ref, src=None):
        k = self.u if axis == self.first else self.v
        return [
            self.mail.post(ref if src is None else src, ref, {axis: fold(k + d)}) for d in (1, N - 1)
        ]

    def along_first(self, src=None):
        self.near = self.both(self.first, self.ref(self.u, self.v, 0), src)

    def plane(self, d, src=None):
        self.planes[d] = self.both(self.second, self.ref(fold(self.u + d), self.v, 0), src)

    def relay_first(self):
        before, after = fold(self.u + N - 1), fold(self.u + 1)
        self.near[0].wait_recv()
        low = self.ref(before, self.v, 1)
        self.far = [self.mail.post(low, low, {self.first: after})]
        self.near[1].wait_recv()
        high = self.ref(after, self.v, 2)
        self.far.append(self.mail.post(high, high, {self.first: before}))

    def far_first(self):
        for copy in self.far:
            copy.wait_recv()

    def relay_second(self, d):
        before, after = fold(self.v + N - 1), fold(self.v + 1)
        p = fold(self.u + d)
        self.planes[d][0].wait_recv()
        low = self.ref(p, before, 1)
        self.relays.append(self.mail.post(low, low, {self.second: after}))
        self.planes[d][1].wait_recv()
        high = self.ref(p, after, 2)
        self.relays.append(self.mail.post(high, high, {self.second: before}))

    def finish(self):
        for copy in self.relays:
            copy.wait_recv()


def advance(gathers, step, sources=None):
    if step == 0:
        for k, g in enumerate(gathers):
            g.along_first(sources and sources[k])
        for k, g in enumerate(gathers):
            g.plane(0, sources and sources[k])
    elif step == 1:
        for g in gathers:
            g.relay_first()
            g.plane(N - 1)
            g.plane(1)
    elif step == 2:
        for g in gathers:
            g.relay_second(0)
        for g in gathers:
            g.far_first()
            g.plane(2)
    elif step == 3:
        for g in gathers:
            g.relay_second(N - 1)
            g.relay_second(1)
    elif step == 4:
        for g in gathers:
            g.relay_second(2)
    else:
        for g in gathers:
            g.finish()


class Reduce:
    def __init__(self, mail, part, boxes, at, first, second, out, columns):
        self.mail, self.part, self.at = mail, part, at
        self.send1, self.recv1, self.mid, self.send2, self.recv2, self.last, self.send3, self.recv3 = boxes
        self.first, self.second = first, second
        self.u, self.w = at[first], at[second]
        self.out, self.columns = out, columns

    def partial(self, u, w, start):
        y, x = (w, u) if self.first == X else (u, w)
        return self.part[y, pl.ds(start, 2), x]

    def post1(self, k, d):
        return self.mail.post(self.send1.at[k], self.recv1.at[k], {self.first: fold(self.u + d)})

    def post2(self, k, d):
        return self.mail.post(self.send2.at[k], self.recv2.at[k], {self.second: fold(self.w + d)})

    def open1(self):
        self.one = []
        plan = ((2, 0, 1), (2, 2, N - 1), (1, 2, 1), (N - 1, 0, N - 1))
        for k, (to, start, d) in enumerate(plan):
            u = fold(self.u + to)

            def stage(w, _):
                self.send1[k, w] = self.partial(u, w, start).astype(BF16)
                return _

            lax.fori_loop(0, N, stage, 0)
            self.one.append(self.post1(k, d))

    def relay1(self):
        for k, to, start in ((0, 1, 0), (1, N - 1, 2)):
            self.one[k].wait_recv()
            u = fold(self.u + to)

            def stage(w, _):
                total = self.partial(u, w, start) + self.recv1[k, w].astype(F32)
                self.send1[4 + k, w] = total.astype(BF16)
                return _

            lax.fori_loop(0, N, stage, 0)
            self.one.append(self.post1(4 + k, to))

    def open2(self):
        for k in (2, 3, 4, 5):
            self.one[k].wait_recv()

        def total(w, _):
            self.mid[w, 0:2] = (
                self.partial(self.u, w, 0) + self.recv1[3, w].astype(F32) + self.recv1[4, w].astype(F32)
            )
            self.mid[w, 2:4] = (
                self.partial(self.u, w, 2) + self.recv1[2, w].astype(F32) + self.recv1[5, w].astype(F32)
            )
            return _

        lax.fori_loop(0, N, total, 0)
        self.two = []
        plan = ((2, 0, 1), (2, 2, N - 1), (1, 2, 1), (N - 1, 0, N - 1))
        for k, (to, start, d) in enumerate(plan):
            self.send2[k] = self.mid[fold(self.w + to), start : start + 2].astype(self.send2.dtype)
            self.two.append(self.post2(k, d))

    def relay2(self):
        for k, to, start in ((0, 1, 0), (1, N - 1, 2)):
            self.two[k].wait_recv()
            total = self.mid[fold(self.w + to), start : start + 2] + self.recv2[k].astype(F32)
            self.send2[4 + k] = total.astype(self.send2.dtype)
            self.two.append(self.post2(4 + k, to))

    def open3(self):
        for k in (2, 3, 4, 5):
            self.two[k].wait_recv()
        self.last[0:2] = self.mid[self.w, 0:2] + self.recv2[3].astype(F32) + self.recv2[4].astype(F32)
        self.last[2:4] = self.mid[self.w, 2:4] + self.recv2[2].astype(F32) + self.recv2[5].astype(F32)
        self.three = []
        for d in (2, 1, N - 1):
            z = fold(self.at[Z] + d)
            self.send3[d - 1] = self.last[z].astype(BF16)
            self.three.append(self.mail.post(self.send3.at[d - 1], self.recv3.at[d - 1], {Z: z}))

    def finish(self):
        total = self.last[self.at[Z]]
        for copy in self.three:
            copy.wait_recv()
        for d in range(1, N):
            total += self.recv3[d - 1].astype(F32)
        self.out[:, self.columns] = total


def kernel(
    hidden, words, targets, embedding_hbm,
    loss, hidden_grad, embed_grad,
    tokens, extra, sibling, embedding, scores, slopes, picks, slopes_t, picks_t, dlogits, by_token, part, plane_sums, depth_sums,
    send1, recv1, mid, send2, recv2, last, send3, recv3,
    load_sem, send_sem, recv_sem,
):
    at = {a: lax.axis_index(a) for a in AXES}
    half, core, y, z, x = (at[a] for a in AXES)
    width = hidden.shape[1]
    vocab_local = embedding.shape[0]
    group = tokens.shape[0] * tokens.shape[1] * tokens.shape[2] * ROWS
    color, share, lane = width // 2, width // 4, width // (2 * LANES)
    partner = {HALF: 1 - half}
    across = {HALF: 1 - half, CORE: 1 - core}
    other = {CORE: 1 - core}
    vocab_start = ((y * N + z) * N + x) * vocab_local

    load = pltpu.make_async_copy(embedding_hbm, embedding, load_sem)
    load.start()
    barrier = pltpu.get_barrier_semaphore()
    plane_peers = [(i, j) for i in range(N) for j in range(N) if i or j]
    greeted = [{Y: fold(y + i), X: fold(x + j)} for i, j in plane_peers]
    greeted += [{Z: fold(z + d)} for d in range(1, N)] + [partner, across, other]
    for device in greeted:
        pl.semaphore_signal(barrier, inc=1, device_id=device, device_id_type=MESH)
    pl.semaphore_wait(barrier, len(greeted))

    mail = Mail(send_sem, recv_sem)
    inner = z * (N - 1 - z) // 2
    nearest, middle = 1 + 2 * (z // 2), 2 + inner * (3 - 2 * z)
    order = (nearest, middle, 6 - nearest - middle)
    own = mail.post_each(hidden, tokens.at[y, z, x], Z, z, order)

    def share_of(h, c):
        return pl.ds(pl.multiple_of((2 * h + c) * share, 128), share)

    def slot(k, start, size):
        half_size = size // 2
        zs = pl.ds(k, 1)
        return (
            (zs, pl.ds(start, size)),
            (zs, pl.ds(start, half_size)),
            (zs, pl.ds(start + half_size, half_size)),
        )

    def main_view(yy, xx, piece):
        return tokens.at[yy, piece[0], xx, :, piece[1]]

    def extra_view(k):
        return lambda yy, xx, piece: extra.at[k, yy, piece[0], xx]

    def main_pair(k):
        return [
            Gather(mail, main_view, at, Y, X, slot(k, 0, color)),
            Gather(mail, main_view, at, X, Y, slot(k, color, color)),
        ]

    tokens[y, z, x] = hidden[...]
    mains = [main_pair(z)] + [main_pair(fold(z + d)) for d in order]
    advance(mains[0], 0)
    crossed = [
        mail.post(hidden.at[:, share_of(1 - half, core)], extra.at[0, y, z, x], partner),
        mail.post(hidden.at[:, share_of(1 - half, 1 - core)], extra.at[1, y, z, x], across),
    ]
    depth = ((pl.ds(0, N),), (pl.ds(0, 2),), (pl.ds(2, 2),))
    extras = [
        Gather(mail, extra_view(0), at, Y, X, depth),
        Gather(mail, extra_view(1), at, X, Y, depth),
    ]
    advance(mains[0], 1)
    own[0].wait_recv()
    advance(mains[1], 0)
    advance(mains[0], 2)
    own[1].wait_recv()
    advance(mains[2], 0)
    advance(mains[1], 1)
    own[2].wait_recv()
    advance(mains[3], 0)
    advance(mains[0], 3)
    advance(mains[2], 1)
    advance(mains[1], 2)
    for copy in crossed:
        copy.wait_recv()
    lifted = mail.post_each(extra.at[:, y, z, x], extra.at[:, y, z, x], Z, z, order)
    advance(mains[3], 1)
    advance(mains[2], 2)
    advance(mains[0], 4)
    advance(mains[1], 3)
    advance(mains[3], 2)
    advance(mains[2], 3)
    advance(mains[1], 4)
    advance(mains[3], 3)
    advance(mains[2], 4)
    for copy in lifted:
        copy.wait_recv()
    advance(mains[3], 4)
    advance(extras, 0)
    for pair in mains:
        advance(pair, 5)
    load.wait()

    to_sibling = mail.post(
        tokens.at[:, :, :, :, share_of(half, 1 - core)], sibling.at[...], other
    )

    block = group // 2

    def score(k):
        rows = tokens[pl.ds(2 * k, 2)].reshape(block, width)
        scores[k] = lax.dot_general(
            embedding[...], rows, (((1,), (1,)), ((), ())), preferred_element_type=F32
        )

    score(0)
    for g in extras:
        g.relay_first()
    score(1)

    def cap(w, carry):
        total, target = carry
        rows = pl.ds(pl.multiple_of(w * 32, 32), 32)
        raw = jnp.concatenate([scores[0, rows], scores[1, rows]], axis=1)
        capped = softcap * jnp.tanh(raw / softcap)
        allowed, onehot = masks(words[pl.ds(w, 1)], targets[...], vocab_start + w * 32)
        weight = jnp.where(allowed, jnp.exp(capped), 0.0)
        total += weight.reshape(4, 8, group).sum(axis=0)
        target += jnp.where(onehot, capped, 0.0).reshape(4, 8, group).sum(axis=0)
        slope = 1.0 - jnp.square(capped / softcap)
        slopes[rows] = weight * slope
        picks[rows] = jnp.where(onehot, slope, 0.0)
        return total, target

    zero = jnp.zeros((8, group), F32)
    total, target = lax.fori_loop(0, vocab_local // 32, cap, (zero, zero))
    total = total.sum(axis=0, keepdims=True)
    target = target.sum(axis=0, keepdims=True)

    def swap(sums, me, peers):
        sums[me, 0:1] = total
        sums[me, 1:2] = target
        return [mail.post(sums.at[me], sums.at[me], device) for device in peers]

    def summed(sums, copies):
        for copy in copies:
            copy.wait_recv()
        both = sums[...].sum(axis=0)
        return both[0:1], both[1:2]

    def turn(k):
        rows = pl.ds(k * 128, 128)
        slopes_t[:, rows] = slopes[rows].T
        picks_t[:, rows] = picks[rows].T

    copies = swap(plane_sums, y * N + x, [{Y: fold(y + i), X: fold(x + j)} for i, j in plane_peers])
    for g in extras:
        g.plane(N - 1)
        g.plane(1)
    for k in range(vocab_local // 128):
        turn(k)
    total, target = summed(plane_sums, copies)
    copies = swap(depth_sums, z, [{Z: fold(z + d)} for d in range(1, N)])
    advance(extras, 2)
    total, target = summed(depth_sums, copies)
    log_total = jnp.log(total)
    loss[...] = log_total - target
    inverse = 1.0 / total
    inverse_t = jnp.broadcast_to(inverse, (128, group)).T

    for k in range(vocab_local // 128):
        columns = pl.ds(k * 128, 128)
        by_token[:, columns] = (slopes_t[:, columns] * inverse_t - picks_t[:, columns]).astype(BF16)

    def by_vocabulary(k, _):
        rows = pl.ds(pl.multiple_of(k * 32, 32), 32)
        dlogits[0, rows] = (slopes[rows] * inverse - picks[rows]).astype(BF16)
        return _

    tile = share // 3

    def product(k):
        step = lane // 2

        def piece(j, _):
            source = pl.ds(pl.multiple_of(k * lane + j * step, 128), step)
            columns = pl.ds(pl.multiple_of(j * step, 128), step)
            value = jnp.dot(by_token[...], embedding[:, source], preferred_element_type=F32)
            part[k, :, :, :, :, columns] = value.reshape(N, N, N, ROWS, step)
            return _

        lax.fori_loop(0, 2, piece, 0)

    def reducer(k, first, second):
        boxes = [b.at[k] for b in (send1, recv1, mid, send2, recv2, last, send3, recv3)]
        return Reduce(mail, part.at[k], boxes, at, first, second, hidden_grad, pl.ds(k * lane, lane))

    lanes = [(k, k + LANES) for k in range(LANES)]
    pairs = [(reducer(i, X, Y), reducer(j, Y, X)) for i, j in lanes]

    def open1(k):
        for i, r in zip(lanes[k], pairs[k]):
            product(i)
            r.open1()

    def run(k, *names):
        for name in names:
            for r in pairs[k]:
                getattr(r, name)()

    def grad(k, source, begin):
        def piece(j, _):
            columns = pl.ds(pl.multiple_of(j * tile, 128), tile)
            value = jnp.dot(
                dlogits[k], source(j).reshape(group, tile), preferred_element_type=F32
            )
            if begin:
                embed_grad[:, columns] = value
            else:
                embed_grad[:, columns] += value
            return _

        lax.fori_loop(0, 3, piece, 0)

    def columns_of(j):
        return pl.ds(pl.multiple_of(j * tile, 128), tile)

    def own_columns(j):
        return pl.ds(pl.multiple_of((2 * half + core) * share + j * tile, 128), tile)

    open1(0)
    lax.fori_loop(0, vocab_local // 32, by_vocabulary, 0)
    around = mail.post(dlogits.at[0], dlogits.at[2], partner)
    beside = mail.post(dlogits.at[0], dlogits.at[1], other)
    run(0, "relay1")
    open1(1)
    grad(0, lambda j: tokens[:, :, :, :, own_columns(j)], True)
    run(1, "relay1")
    run(0, "open2")
    open1(2)
    run(0, "relay2")
    run(2, "relay1")
    run(1, "open2")
    run(0, "open3")
    beside.wait_recv()
    to_sibling.wait_recv()
    grad(1, lambda j: sibling[:, :, :, :, columns_of(j)], False)
    run(2, "open2")
    advance(extras, 3)
    run(1, "relay2")
    around.wait_recv()
    passed = mail.post(dlogits.at[2], dlogits.at[3], other)
    run(2, "relay2")
    advance(extras, 4)
    run(1, "open3")
    run(2, "open3")
    advance(extras, 5)
    grad(2, lambda j: extra[0, :, :, :, :, columns_of(j)], False)
    passed.wait_recv()
    grad(3, lambda j: extra[1, :, :, :, :, columns_of(j)], False)
    for k in range(LANES):
        run(k, "finish")
    mail.close()


def write_out(loss, hidden_grad, embed_grad, loss_out, hidden_out, embed_out, sem):
    pairs = ((hidden_grad, hidden_out), (embed_grad, embed_out))
    copies = [pltpu.make_async_copy(a, b, sem.at[k]) for k, (a, b) in enumerate(pairs)]
    for copy in copies:
        copy.start()
    loss_out[...] = loss[0]
    for copy in copies:
        copy.wait()


def on_device(hidden, embedding, targets, grammar_bits):
    rows, width = hidden.shape
    vocab_local = embedding.shape[0]
    group = targets.shape[0]
    share, lane, lanes = width // 4, width // (2 * LANES), 2 * LANES
    vmem = pl.BlockSpec(memory_space=pltpu.VMEM)
    blocks = (N, N, N, ROWS)
    hbm = pl.BlockSpec(memory_space=pltpu.HBM)
    results = pl.pallas_call(
        kernel,
        out_shape=(
            jax.ShapeDtypeStruct((1, group), F32),
            jax.ShapeDtypeStruct((rows, width), F32),
            jax.ShapeDtypeStruct((vocab_local, share), F32),
        ),
        in_specs=[vmem, vmem, vmem, hbm],
        out_specs=(vmem, vmem, vmem),
        scratch_shapes=[
            pltpu.VMEM(blocks + (width,), BF16),
            pltpu.VMEM((2,) + blocks + (share,), BF16),
            pltpu.VMEM(blocks + (share,), BF16),
            pltpu.VMEM((vocab_local, width), BF16),
            pltpu.VMEM((2, vocab_local, group // 2), F32),
            pltpu.VMEM((vocab_local, group), F32),
            pltpu.VMEM((vocab_local, group), F32),
            pltpu.VMEM((group, vocab_local), F32),
            pltpu.VMEM((group, vocab_local), F32),
            pltpu.VMEM((4, vocab_local, group), BF16),
            pltpu.VMEM((group, vocab_local), BF16),
            pltpu.VMEM((lanes,) + blocks + (lane,), F32),
            pltpu.VMEM((N * N, 2, group), F32),
            pltpu.VMEM((N, 2, group), F32),
            pltpu.VMEM((lanes, 6, N, 2, ROWS, lane), BF16),
            pltpu.VMEM((lanes, 6, N, 2, ROWS, lane), BF16),
            pltpu.VMEM((lanes, N, N, ROWS, lane), F32),
            pltpu.VMEM((lanes, 6, 2, ROWS, lane), F32),
            pltpu.VMEM((lanes, 6, 2, ROWS, lane), F32),
            pltpu.VMEM((lanes, N, ROWS, lane), F32),
            pltpu.VMEM((lanes, N - 1, ROWS, lane), BF16),
            pltpu.VMEM((lanes, N - 1, ROWS, lane), BF16),
            pltpu.SemaphoreType.DMA,
            pltpu.SemaphoreType.DMA((340,)),
            pltpu.SemaphoreType.DMA((340,)),
        ],
        compiler_params=pltpu.CompilerParams(
            collective_id=0, has_side_effects=True, vmem_limit_bytes=50 * 1024 * 1024
        ),
        name="fused",
    )(hidden, grammar_bits.T, targets[None, :], embedding)
    return pl.pallas_call(
        write_out,
        out_shape=(
            jax.ShapeDtypeStruct((group,), F32),
            jax.ShapeDtypeStruct((rows, width), F32),
            jax.ShapeDtypeStruct((vocab_local, share), F32),
        ),
        in_specs=[vmem, vmem, vmem],
        out_specs=(vmem, hbm, hbm),
        scratch_shapes=[pltpu.SemaphoreType.DMA((2,))],
        compiler_params=pltpu.CompilerParams(vmem_limit_bytes=8 * 1024 * 1024),
        name="write_out",
    )(*results)


def solution(mesh):
    split = Mesh(mesh.devices.reshape(2, 2, 4, 4, 4), AXES)
    return jax.shard_map(
        on_device,
        mesh=split,
        in_specs=(P(AXES, None), P(VOCAB, None), P(DP), P(DP, VOCAB)),
        out_specs=(P(DP), P(AXES, None), P(VOCAB, DP)),
        check_vma=False,
    )
```

time: 120 us -> 105 us (0.88)
  Pallas kernels: 113 us -> 102 us
  local copies, waits for them, and re-layouts: 6.04 us -> 2.32 us
    pallas_call x1, Pallas kernels: 113 us -> 99.8 us  [on_device(): pl.pallas_call(kernel, out_shape=(jax.ShapeDtypeStruct((1, group), F32),...]
    unnamed x3 -> x6, local copies, waits for them, and re-layouts: 6.04 us -> 2.32 us
    pallas_call x0 -> x1, Pallas kernels: none -> 2.05 us  [on_device(): pl.pallas_call(write_out, out_shape=(jax.ShapeDtypeStruct((group,), F32),...]
where the time goes in v2:
time: 105 us
  Pallas kernels  102 us (97%)
  local copies, waits for them, and re-layouts  2.32 us (2%)
    pallas_call x1, Pallas kernels, on_device(): pl.pallas_call(kernel, out_shape=(jax.ShapeDtypeStruct((1, group), F32),...  99.8 us
    unnamed x6, local copies, waits for them, and re-layouts  2.32 us

profile of v2, /device:TPU:2, one launch (start us, length us, event | category | flops | bytes accessed | tf_op | source)
XLA Modules:
  0.0 104.8 jit_solution(2832116552155360490)
XLA Ops:
  0.6 0.0 copy-start
  0.6 0.9 copy-done
  1.5 0.0 copy-start.1
  1.5 0.8 copy-done.1
  2.3 0.0 copy-start.2
  2.3 0.7 copy-done.2
  3.0 99.8 %fused.1 = (f32[1,512]{1,0:T(1,128)S(1)}, f32[8,4608]{1,0:T(8,128)S(1)}, f32[512,1152]{1,0:T(8,128)S(1)}) custom-call(bf16[8,4608]{1,0:T(8,128)(2,1)S(1)} %copy-done, s32[16,512]{1,0:T(8,128)S(1)} %bitcast.2, s32[1,512]{1,0:T(1,128)S(1)} %bitcast.3, bf16[512,4608]{1,0:T(8,128)(2,1)} %embedding_hbm.1), custom_call_target="tpu_custom_call" | custom-call | tf_op jit(solution)/shard_map/fused/pallas_call | solution.py:529
  102.8 2.1 %write_out.1 = (f32[512]{0:T(512)}, f32[8,4608]{1,0:T(8,128)}, f32[512,1152]{1,0:T(8,128)}) custom-call(f32[1,512]{1,0:T(1,128)S(1)} %get-tuple-element.6.loss, f32[8,4608]{1,0:T(8,128)S(1)} %get-tuple-element.7.hidden_grad, f32[512,1152]{1,0:T(8,128)S(1)} %get-tuple-element.8.embed_grad), custom_call_target="tpu_custom_call" | custom-call | tf_op jit(solution)/shard_map/write_out/pallas_call | solution.py:570
Async XLA Ops:
  0.6 0.9 copy-start
  1.5 0.8 copy-start.1
  2.3 0.7 copy-start.2

commit v3 on v2

--- a/solution.py
+++ b/solution.py
@@ -247,7 +247,7 @@
 def kernel(
     hidden, words, targets, embedding_hbm,
     loss, hidden_grad, embed_grad,
-    tokens, extra, sibling, embedding, scores, slopes, picks, slopes_t, picks_t, dlogits, by_token, part, plane_sums, depth_sums,
+    tokens, extra, sibling, embedding, embedding_t, scores, slopes, picks, slopes_t, picks_t, dlogits, by_token, part, plane_sums, depth_sums,
     send1, recv1, mid, send2, recv2, last, send3, recv3,
     load_sem, send_sem, recv_sem,
 ):
@@ -304,6 +304,16 @@
 
     tokens[y, z, x] = hidden[...]
     mains = [main_pair(z)] + [main_pair(fold(z + d)) for d in order]
+    def flip(part):
+        blocks = width // 256
+
+        def piece(k, _):
+            span = pl.ds(pl.multiple_of((part * blocks + k) * 128, 128), 128)
+            embedding_t[span, :] = embedding[:, span].T
+            return _
+
+        lax.fori_loop(0, blocks, piece, 0)
+
     advance(mains[0], 0)
     crossed = [
         mail.post(hidden.at[:, share_of(1 - half, core)], extra.at[0, y, z, x], partner),
@@ -318,24 +328,27 @@
     own[0].wait_recv()
     advance(mains[1], 0)
     advance(mains[0], 2)
+    advance(mains[1], 1)
+    load.wait()
+    flip(0)
     own[1].wait_recv()
     advance(mains[2], 0)
-    advance(mains[1], 1)
+    advance(mains[0], 3)
     own[2].wait_recv()
     advance(mains[3], 0)
-    advance(mains[0], 3)
-    advance(mains[2], 1)
     advance(mains[1], 2)
     for copy in crossed:
         copy.wait_recv()
     lifted = mail.post_each(extra.at[:, y, z, x], extra.at[:, y, z, x], Z, z, order)
+    advance(mains[2], 1)
+    advance(mains[0], 4)
     advance(mains[3], 1)
+    advance(mains[1], 3)
+    flip(1)
     advance(mains[2], 2)
-    advance(mains[0], 4)
-    advance(mains[1], 3)
+    advance(mains[1], 4)
     advance(mains[3], 2)
     advance(mains[2], 3)
-    advance(mains[1], 4)
     advance(mains[3], 3)
     advance(mains[2], 4)
     for copy in lifted:
@@ -344,30 +357,25 @@
     advance(extras, 0)
     for pair in mains:
         advance(pair, 5)
-    load.wait()
 
     to_sibling = mail.post(
         tokens.at[:, :, :, :, share_of(half, 1 - core)], sibling.at[...], other
     )
 
-    block = group // 2
-
-    def score(k):
-        rows = tokens[pl.ds(2 * k, 2)].reshape(block, width)
-        scores[k] = lax.dot_general(
-            embedding[...], rows, (((1,), (1,)), ((), ())), preferred_element_type=F32
-        )
-
-    score(0)
-    for g in extras:
-        g.relay_first()
-    score(1)
+    def score(k, _):
+        span = pl.ds(pl.multiple_of(k * 256, 256), 256)
+        rows = tokens[...].reshape(group, width)
+        value = jnp.dot(rows, embedding_t[:, span], preferred_element_type=F32)
+        scores[span, :] = value.T
+        return _
+
+    advance(extras, 1)
+    lax.fori_loop(0, vocab_local // 256, score, 0)
 
     def cap(w, carry):
         total, target = carry
         rows = pl.ds(pl.multiple_of(w * 32, 32), 32)
-        raw = jnp.concatenate([scores[0, rows], scores[1, rows]], axis=1)
-        capped = softcap * jnp.tanh(raw / softcap)
+        capped = softcap * jnp.tanh(scores[rows] / softcap)
         allowed, onehot = masks(words[pl.ds(w, 1)], targets[...], vocab_start + w * 32)
         weight = jnp.where(allowed, jnp.exp(capped), 0.0)
         total += weight.reshape(4, 8, group).sum(axis=0)
@@ -399,14 +407,12 @@
         picks_t[:, rows] = picks[rows].T
 
     copies = swap(plane_sums, y * N + x, [{Y: fold(y + i), X: fold(x + j)} for i, j in plane_peers])
-    for g in extras:
-        g.plane(N - 1)
-        g.plane(1)
     for k in range(vocab_local // 128):
         turn(k)
+    advance(extras, 2)
     total, target = summed(plane_sums, copies)
     copies = swap(depth_sums, z, [{Z: fold(z + d)} for d in range(1, N)])
-    advance(extras, 2)
+    advance(extras, 3)
     total, target = summed(depth_sums, copies)
     log_total = jnp.log(total)
     loss[...] = log_total - target
@@ -422,19 +428,11 @@
         dlogits[0, rows] = (slopes[rows] * inverse - picks[rows]).astype(BF16)
         return _
 
-    tile = share // 3
-
     def product(k):
-        step = lane // 2
-
-        def piece(j, _):
-            source = pl.ds(pl.multiple_of(k * lane + j * step, 128), step)
-            columns = pl.ds(pl.multiple_of(j * step, 128), step)
-            value = jnp.dot(by_token[...], embedding[:, source], preferred_element_type=F32)
-            part[k, :, :, :, :, columns] = value.reshape(N, N, N, ROWS, step)
-            return _
-
-        lax.fori_loop(0, 2, piece, 0)
+        value = jnp.dot(
+            by_token[...], embedding[:, pl.ds(k * lane, lane)], preferred_element_type=F32
+        )
+        part[k] = value.reshape(N, N, N, ROWS, lane)
 
     def reducer(k, first, second):
         boxes = [b.at[k] for b in (send1, recv1, mid, send2, recv2, last, send3, recv3)]
@@ -454,55 +452,41 @@
                 getattr(r, name)()
 
     def grad(k, source, begin):
-        def piece(j, _):
-            columns = pl.ds(pl.multiple_of(j * tile, 128), tile)
-            value = jnp.dot(
-                dlogits[k], source(j).reshape(group, tile), preferred_element_type=F32
-            )
-            if begin:
-                embed_grad[:, columns] = value
-            else:
-                embed_grad[:, columns] += value
-            return _
-
-        lax.fori_loop(0, 3, piece, 0)
-
-    def columns_of(j):
-        return pl.ds(pl.multiple_of(j * tile, 128), tile)
-
-    def own_columns(j):
-        return pl.ds(pl.multiple_of((2 * half + core) * share + j * tile, 128), tile)
+        value = jnp.dot(dlogits[k], source.reshape(group, share), preferred_element_type=F32)
+        if begin:
+            embed_grad[...] = value
+        else:
+            embed_grad[...] += value
 
     open1(0)
     lax.fori_loop(0, vocab_local // 32, by_vocabulary, 0)
     around = mail.post(dlogits.at[0], dlogits.at[2], partner)
     beside = mail.post(dlogits.at[0], dlogits.at[1], other)
+    open1(1)
+    advance(extras, 4)
     run(0, "relay1")
-    open1(1)
-    grad(0, lambda j: tokens[:, :, :, :, own_columns(j)], True)
+    open1(2)
     run(1, "relay1")
+    grad(0, tokens[:, :, :, :, share_of(half, core)], True)
     run(0, "open2")
-    open1(2)
-    run(0, "relay2")
     run(2, "relay1")
-    run(1, "open2")
-    run(0, "open3")
     beside.wait_recv()
     to_sibling.wait_recv()
-    grad(1, lambda j: sibling[:, :, :, :, columns_of(j)], False)
+    grad(1, sibling[...], False)
+    run(1, "open2")
+    run(0, "relay2")
     run(2, "open2")
-    advance(extras, 3)
     run(1, "relay2")
+    run(0, "open3")
     around.wait_recv()
     passed = mail.post(dlogits.at[2], dlogits.at[3], other)
     run(2, "relay2")
-    advance(extras, 4)
     run(1, "open3")
     run(2, "open3")
     advance(extras, 5)
-    grad(2, lambda j: extra[0, :, :, :, :, columns_of(j)], False)
+    grad(2, extra[0], False)
     passed.wait_recv()
-    grad(3, lambda j: extra[1, :, :, :, :, columns_of(j)], False)
+    grad(3, extra[1], False)
     for k in range(LANES):
         run(k, "finish")
     mail.close()
@@ -540,7 +524,8 @@
             pltpu.VMEM((2,) + blocks + (share,), BF16),
             pltpu.VMEM(blocks + (share,), BF16),
             pltpu.VMEM((vocab_local, width), BF16),
-            pltpu.VMEM((2, vocab_local, group // 2), F32),
+            pltpu.VMEM((width, vocab_local), BF16),
+            pltpu.VMEM((vocab_local, group), F32),
             pltpu.VMEM((vocab_local, group), F32),
             pltpu.VMEM((vocab_local, group), F32),
             pltpu.VMEM((group, vocab_local), F32),

time: 105 us -> 102 us (0.971)
  Pallas kernels: 102 us -> 98.9 us
    pallas_call x1, Pallas kernels: 99.8 us -> 96.8 us  [on_device(): pl.pallas_call(kernel, out_shape=(jax.ShapeDtypeStruct((1, group), F32),...]
where the time goes in v3:
time: 102 us
  Pallas kernels  98.9 us (97%)
  local copies, waits for them, and re-layouts  2.32 us (2%)
    pallas_call x1, Pallas kernels, on_device(): pl.pallas_call(kernel, out_shape=(jax.ShapeDtypeStruct((1, group), F32),...  96.8 us
    unnamed x6, local copies, waits for them, and re-layouts  2.32 us
    pallas_call x1, Pallas kernels, on_device(): pl.pallas_call(write_out, out_shape=(jax.ShapeDtypeStruct((group,), F32),...  2.05 us

profile of v3, /device:TPU:2, one launch (start us, length us, event | category | flops | bytes accessed | tf_op | source)
XLA Modules:
  0.0 101.8 jit_solution(6125756338937046791)
XLA Ops:
  0.6 0.0 copy-start
  0.6 0.9 copy-done
  1.5 0.0 copy-start.1
  1.5 0.8 copy-done.1
  2.3 0.0 copy-start.2
  2.3 0.7 copy-done.2
  3.0 96.8 %fused.1 = (f32[1,512]{1,0:T(1,128)S(1)}, f32[8,4608]{1,0:T(8,128)S(1)}, f32[512,1152]{1,0:T(8,128)S(1)}) custom-call(bf16[8,4608]{1,0:T(8,128)(2,1)S(1)} %copy-done, s32[16,512]{1,0:T(8,128)S(1)} %bitcast.2, s32[1,512]{1,0:T(1,128)S(1)} %bitcast.3, bf16[512,4608]{1,0:T(8,128)(2,1)} %embedding_hbm.1), custom_call_target="tpu_custom_call" | custom-call | tf_op jit(solution)/shard_map/fused/pallas_call | solution.py:513
  99.8 2.1 %write_out.1 = (f32[512]{0:T(512)}, f32[8,4608]{1,0:T(8,128)}, f32[512,1152]{1,0:T(8,128)}) custom-call(f32[1,512]{1,0:T(1,128)S(1)} %get-tuple-element.6.loss, f32[8,4608]{1,0:T(8,128)S(1)} %get-tuple-element.7.hidden_grad, f32[512,1152]{1,0:T(8,128)S(1)} %get-tuple-element.8.embed_grad), custom_call_target="tpu_custom_call" | custom-call | tf_op jit(solution)/shard_map/write_out/pallas_call | solution.py:555
Async XLA Ops:
  0.6 0.9 copy-start
  1.5 0.8 copy-start.1
  2.3 0.7 copy-start.2

commit v4 on v3

--- a/solution.py
+++ b/solution.py
@@ -67,9 +67,11 @@
             self.start(self.describe(src, dst, {axis: fold(me + d)}, base + d, base + N - d))
         return [self.describe(src, dst, {axis: fold(me + d)}, base + d, base + d) for d in steps]
 
-    def close(self):
-        for copy in self.sent:
+    def close(self, spare=0):
+        done = len(self.sent) - spare
+        for copy in self.sent[:done]:
             copy.wait_send()
+        self.sent = self.sent[done:]
 
 
 class Gather:
@@ -480,15 +482,17 @@
     run(0, "open3")
     around.wait_recv()
     passed = mail.post(dlogits.at[2], dlogits.at[3], other)
+    advance(extras, 5)
+    grad(2, extra[0], False)
     run(2, "relay2")
     run(1, "open3")
-    run(2, "open3")
-    advance(extras, 5)
-    grad(2, extra[0], False)
     passed.wait_recv()
     grad(3, extra[1], False)
-    for k in range(LANES):
-        run(k, "finish")
+    run(2, "open3")
+    run(0, "finish")
+    run(1, "finish")
+    mail.close(2 * 2 * (N - 1))
+    run(2, "finish")
     mail.close()
 
 

time: 102 us -> 102 us (level)
  no operation moved by 1% of the time
where the time goes in v4:
time: 102 us; the launch traced here: 101 us
  Pallas kernels  98.4 us (96%)
  local copies, waits for them, and re-layouts  2.32 us (2%)
    pallas_call x1, Pallas kernels, on_device(): pl.pallas_call(kernel, out_shape=(jax.ShapeDtypeStruct((1, group), F32),...  96.3 us
    unnamed x6, local copies, waits for them, and re-layouts  2.32 us
    pallas_call x1, Pallas kernels, on_device(): pl.pallas_call(write_out, out_shape=(jax.ShapeDtypeStruct((group,), F32),...  2.05 us

profile of v4, /device:TPU:2, one launch (start us, length us, event | category | flops | bytes accessed | tf_op | source)
XLA Modules:
  0.0 101.3 jit_solution(1348228560299281218)
XLA Ops:
  0.6 0.0 copy-start
  0.6 0.9 copy-done
  1.5 0.0 copy-start.1
  1.5 0.8 copy-done.1
  2.3 0.0 copy-start.2
  2.3 0.7 copy-done.2
  3.0 96.3 %fused.1 = (f32[1,512]{1,0:T(1,128)S(1)}, f32[8,4608]{1,0:T(8,128)S(1)}, f32[512,1152]{1,0:T(8,128)S(1)}) custom-call(bf16[8,4608]{1,0:T(8,128)(2,1)S(1)} %copy-done, s32[16,512]{1,0:T(8,128)S(1)} %bitcast.2, s32[1,512]{1,0:T(1,128)S(1)} %bitcast.3, bf16[512,4608]{1,0:T(8,128)(2,1)} %embedding_hbm.1), custom_call_target="tpu_custom_call" | custom-call | tf_op jit(solution)/shard_map/fused/pallas_call | solution.py:517
  99.3 2.1 %write_out.1 = (f32[512]{0:T(512)}, f32[8,4608]{1,0:T(8,128)}, f32[512,1152]{1,0:T(8,128)}) custom-call(f32[1,512]{1,0:T(1,128)S(1)} %get-tuple-element.6.loss, f32[8,4608]{1,0:T(8,128)S(1)} %get-tuple-element.7.hidden_grad, f32[512,1152]{1,0:T(8,128)S(1)} %get-tuple-element.8.embed_grad), custom_call_target="tpu_custom_call" | custom-call | tf_op jit(solution)/shard_map/write_out/pallas_call | solution.py:559
Async XLA Ops:
  0.6 0.9 copy-start
  1.5 0.8 copy-start.1
  2.3 0.7 copy-start.2
